TPU v7x, 32 devices: a whole 2x2x4 slice. The times are simulated.
32 devices in a mesh: surf: 8 (over y, x, core), probe: 4 (over z).
Axes of the slice: x: 2, y: 2, z: 4, core: 2. Of those that a mesh axis runs over, the one named last changes fastest.
Arguments:
- probes: bfloat16 [32, 65536], P('probe', 'surf'), may hold values from -6 to 6
- sigma: float32 [65536], P('surf'), may hold values from 0.5 to 2
- prior_patch: bfloat16 [128, 128], replicated, may hold values from -0.5 to 0.5
- owner_map: int32 [1024], P('surf'), may hold values from 0 to 7, as said below
- block_perm: int32 [1024], P('surf'), may hold values from 0 to 127, as said below
- col_counts: int32 [1024], P('surf'), may hold values from 1 to 64
- coef: bfloat16 [1024, 1024], P('surf'), may hold values from 0.5 to 1.5
- obs_weight: bfloat16 [1024, 64], P('surf'), may hold values from 0.25 to 1
- column_op: bfloat16 [1024, 1024], replicated, may hold values from -0.1875 to 0.1875
Outputs:
- hess: float32 [32, 65536], P('probe', 'surf')
- diag_est: float32 [65536], P('surf')
- quad: float32 [32], P('probe')
Inputs may be any that keep to these rules, and one draw needn't show every extreme that they name: `owner_map`: the 128 blocks of each surface device go to 8 different column owners, 16 to each. The pairs (owner_map, block_perm) name every slot of every column owner exactly once; a column owner receives 16 blocks from each of 8 surface devices.
All inputs are finite; a program needn't handle non-finite values.
Results may differ from a plain program's by a relative error of at most 0.005.
Values may be sent and summed in bfloat16 or wider, within the bound.
A program may use at most 64 MiB of HBM per device.

v0:
```python
import functools

import jax
import jax.numpy as jnp
from jax import lax
from jax.experimental import pallas as pl
from jax.experimental.pallas import tpu as pltpu
from jax.sharding import PartitionSpec as P

F32 = jnp.float32
BF16 = jnp.bfloat16
NT = (((1,), (1,)), ((), ()))
CHUNKS = 1


def kernel(
    n, z, total_probes,
    owner_hbm, slot_hbm, count_hbm, obs_hbm, patch_hbm, sigma_hbm, probes_hbm, coef_hbm, op_hbm,
    hess_ref, diag_ref, quad_ref,
    owner_ref, slot_ref, count_ref, obs_ref, patch_ref, sigma_ref, probes_ref,
    op_ref, ext_ref, ask_out, ask_in, row_out, row_in, coef_ref, weight_ref, spread_ref, lift_ref, diag_in, quad_in,
    load_sem, ask_send, ask_recv, row_send, row_recv, diag_send, diag_recv, quad_send, quad_recv,
):
    width, nodes = probes_ref.shape
    blocks, vol = coef_hbm.shape
    cols = obs_ref.shape[0]
    patch = patch_ref.shape[0]
    groups = nodes // patch
    depth = blocks // n
    me = lax.axis_index("surf")
    zme = lax.axis_index("probe")
    barrier = pltpu.get_barrier_semaphore()

    def surf_peer(i):
        return lax.rem(me + i, n)

    def probe_peer(i):
        return lax.rem(zme + i, z)

    def greet(i, c):
        pl.semaphore_signal(barrier, inc=1, device_id={"surf": surf_peer(i)}, device_id_type=pl.DeviceIdType.MESH)
        return c

    def greet_z(i, c):
        pl.semaphore_signal(barrier, inc=1, device_id={"probe": probe_peer(i)}, device_id_type=pl.DeviceIdType.MESH)
        return c

    lax.fori_loop(1, n, greet, 0)
    lax.fori_loop(1, z, greet_z, 0)

    smalls = (
        (owner_hbm, owner_ref), (slot_hbm, slot_ref), (count_hbm, count_ref), (obs_hbm, obs_ref),
        (patch_hbm, patch_ref), (sigma_hbm, sigma_ref), (probes_hbm, probes_ref),
    )
    loads = [pltpu.make_async_copy(src, dst, load_sem.at[i]) for i, (src, dst) in enumerate(smalls)]
    load_coef = pltpu.make_async_copy(coef_hbm, ext_ref.at[:, pl.ds(0, vol)], load_sem.at[7])
    load_op = pltpu.make_async_copy(op_hbm, op_ref, load_sem.at[8])
    for load in loads + [load_coef, load_op]:
        load.start()
    for load in loads[:4]:
        load.wait()

    square = (blocks, blocks)
    down = lax.broadcasted_iota(jnp.int32, square, 0)
    across = lax.broadcasted_iota(jnp.int32, square, 1)
    owner = jnp.broadcast_to(owner_ref[...], square).astype(F32)
    same = (owner == jnp.transpose(owner)) & (down < across)
    rank = jnp.sum(jnp.where(same, 1.0, 0.0), axis=0, keepdims=True)
    position = owner * depth + rank
    chosen = position == down.astype(F32)
    slots = jnp.broadcast_to(slot_ref[...], square).astype(F32)
    asked = jnp.sum(jnp.where(chosen, slots, 0.0), axis=1, keepdims=True)
    mine = across == me * depth + lax.rem(down, depth)
    asked = jnp.where(mine, jnp.broadcast_to(asked, square), 0.0).astype(jnp.int32)
    ask_out[...] = jnp.sum(asked.reshape(n, depth, blocks), axis=1, keepdims=True)
    ask_in[pl.ds(me, 1)] = ask_out[pl.ds(me, 1)]
    order = (jnp.transpose(position) == across.astype(F32)).astype(F32).astype(BF16)
    counts = jnp.transpose(jnp.broadcast_to(count_ref[...], square).astype(F32))
    lane = lax.broadcasted_iota(jnp.int32, (blocks, patch), 1)
    keep = jnp.where(lax.rem(lane, cols).astype(F32) < counts, 1.0, 0.0)
    twice = (
        lax.rem(lax.broadcasted_iota(jnp.int32, (cols, patch), 1), cols)
        == lax.broadcasted_iota(jnp.int32, (cols, patch), 0)
    ).astype(F32).astype(BF16)
    ext_ref[:, vol:] = lax.dot_general(
        obs_ref[...], twice, (((0,), (0,)), ((), ())), preferred_element_type=F32
    ).astype(BF16)

    pl.semaphore_wait(barrier, (n - 1) + (z - 1))

    def ask(i):
        return pltpu.make_async_remote_copy(
            src_ref=ask_out.at[surf_peer(i)],
            dst_ref=ask_in.at[me],
            send_sem=ask_send.at[i],
            recv_sem=ask_recv.at[i],
            device_id={"surf": surf_peer(i)},
            device_id_type=pl.DeviceIdType.MESH,
        )

    def row(i):
        return pltpu.make_async_remote_copy(
            src_ref=row_out.at[surf_peer(i)],
            dst_ref=row_in.at[me],
            send_sem=row_send.at[i],
            recv_sem=row_recv.at[i],
            device_id={"surf": surf_peer(i)},
            device_id_type=pl.DeviceIdType.MESH,
        )

    def quad_copy(i):
        return pltpu.make_async_remote_copy(
            src_ref=quad_in.at[me],
            dst_ref=quad_in.at[me],
            send_sem=quad_send.at[i],
            recv_sem=quad_recv.at[i],
            device_id={"surf": surf_peer(i)},
            device_id_type=pl.DeviceIdType.MESH,
        )

    per = groups // CHUNKS

    def diag_copy(c, i):
        part = pl.ds(pl.multiple_of(c * per, per), per)
        return pltpu.make_async_remote_copy(
            src_ref=diag_in.at[zme, part],
            dst_ref=diag_in.at[zme, part],
            send_sem=diag_send.at[c, i],
            recv_sem=diag_recv.at[c, i],
            device_id={"probe": probe_peer(i)},
            device_id_type=pl.DeviceIdType.MESH,
        )

    def each(lo, hi, f):
        def step(i, c):
            f(i)
            return c

        lax.fori_loop(lo, hi, step, 0)

    each(1, n, lambda i: ask(i).start())

    for load in loads[4:]:
        load.wait()
    values = probes_ref[...].astype(F32)
    stacked = jnp.concatenate([values[:, k * patch:(k + 1) * patch] for k in range(groups)], axis=0)
    mixed = jnp.dot(stacked.astype(BF16), patch_ref[...], preferred_element_type=F32)
    for k in range(groups):
        spread_ref[k] = (mixed[k * width:(k + 1) * width] * sigma_ref[k:k + 1, :]).astype(BF16).astype(F32)

    load_coef.wait()
    each(1, n, lambda i: ask(i).wait_recv())
    wanted = jnp.broadcast_to(jnp.sum(ask_in[...], axis=0), square).astype(F32)
    pick = (jnp.transpose(wanted) == across.astype(F32)).astype(F32).astype(BF16)
    rows = jnp.dot(pick, ext_ref[...], preferred_element_type=F32).astype(BF16)
    row_out[...] = rows.reshape(row_out.shape)
    row_in[pl.ds(me, 1)] = row_out[pl.ds(me, 1)]
    each(1, n, lambda i: row(i).start())
    each(1, n, lambda i: ask(i).wait_send())
    load_op.wait()
    each(1, n, lambda i: row(i).wait_recv())
    mine = jnp.dot(order, row_in[...].reshape(blocks, row_in.shape[2]), preferred_element_type=F32)
    for t in range(vol // patch):
        coef_ref[:, t * patch:(t + 1) * patch] = mine[:, t * patch:(t + 1) * patch] * keep
    weight_ref[...] = mine[:, vol:]

    low = lax.broadcasted_iota(jnp.int32, (width, patch), 1) < cols
    tiles = vol // patch

    def chunk(c, energy):
        rows_of = 2 * per
        coef_at = coef_ref[pl.ds(pl.multiple_of(c * rows_of, rows_of), rows_of), :]
        weight_at = weight_ref[pl.ds(pl.multiple_of(c * rows_of, rows_of), rows_of), :]
        sigma_at = sigma_ref[pl.ds(pl.multiple_of(c * per, per), per), :]
        for g in range(per):
            k = c * per + g
            field = spread_ref[k]
            turned = pltpu.roll(field, cols, 1)
            pair = (jnp.where(low, field, turned), jnp.where(low, turned, field))
            for half in range(2):
                spot = slice(2 * g + half, 2 * g + half + 1)
                at = (2 * g + half) * width
                for t in range(tiles):
                    span = slice(t * patch, (t + 1) * patch)
                    lift_ref[at:at + width, span] = pair[half] * coef_at[spot, span]
        state = jnp.dot(lift_ref[...].astype(BF16), op_ref[...], preferred_element_type=F32)
        parts = []
        for g in range(2 * per):
            obs_row = weight_at[g:g + 1, :]
            obs_row = jnp.concatenate([jnp.broadcast_to(obs_row, (width, patch))] * tiles, axis=1)
            parts.append(state[g * width:(g + 1) * width] * obs_row)
        weighted = jnp.concatenate(parts, axis=0).astype(BF16)
        adjoint = lax.dot_general(weighted, op_ref[...], NT, preferred_element_type=F32)
        scaled = []
        for g in range(per):
            folded = []
            for half in range(2):
                at = (2 * g + half) * width
                spot = slice(2 * g + half, 2 * g + half + 1)
                total = None
                for t in range(tiles):
                    span = slice(t * patch, (t + 1) * patch)
                    term = adjoint[at:at + width, span] * coef_at[spot, span]
                    total = term if total is None else total + term
                folded.append(total + pltpu.roll(total, cols, 1))
            scaled.append(jnp.where(low, folded[0], folded[1]) * sigma_at[g:g + 1, :])
        scaled = jnp.concatenate(scaled, axis=0)
        high = scaled.astype(BF16)
        rest = (scaled - high.astype(F32)).astype(BF16)
        back = lax.dot_general(high, patch_ref[...], NT, preferred_element_type=F32) + lax.dot_general(
            rest, patch_ref[...], NT, preferred_element_type=F32
        )
        lines = []
        for g in range(per):
            k = c * per + g
            span = pl.ds(pl.multiple_of(k * patch, patch), patch)
            value = probes_ref[:, span].astype(F32)
            term = back[g * width:(g + 1) * width]
            hess_ref[:, span] = value + term
            product = value * term
            energy = energy + product
            lines.append(jnp.sum(product, axis=0, keepdims=True))
        diag_in[zme, pl.ds(pl.multiple_of(c * per, per), per), :] = jnp.concatenate(lines, axis=0)
        each(1, z, lambda i: diag_copy(c, i).start())
        return energy

    energy = lax.fori_loop(0, CHUNKS, chunk, jnp.zeros((width, patch), F32))
    quad_in[me] = energy
    each(1, n, lambda i: quad_copy(i).start())
    each(1, n, lambda i: row(i).wait_send())
    each(0, CHUNKS, lambda c: each(1, z, lambda i: diag_copy(c, i).wait_recv()))
    total = diag_in[0]
    for i in range(1, z):
        total = total + diag_in[i]
    diag_ref[...] = total * (1.0 / total_probes)
    each(1, n, lambda i: quad_copy(i).wait_recv())
    energy = lax.fori_loop(1, n, lambda i, s: s + quad_in[i], quad_in[0])
    energy = jnp.broadcast_to(jnp.sum(energy, axis=1, keepdims=True), (width, patch))
    diagonal = lax.broadcasted_iota(jnp.int32, (width, patch), 0) == lax.broadcasted_iota(jnp.int32, (width, patch), 1)
    quad_ref[...] = jnp.sum(jnp.where(diagonal, energy, 0.0), axis=0, keepdims=True)[:, :width]
    each(0, CHUNKS, lambda c: each(1, z, lambda i: diag_copy(c, i).wait_send()))
    each(1, n, lambda i: quad_copy(i).wait_send())


def settle(hess_in, diag_in, quad_in, hess_out, diag_out, quad_out, hess_at, diag_at, quad_at, sem):
    stops = ((hess_in, hess_at, hess_out), (diag_in, diag_at, diag_out), (quad_in, quad_at, quad_out))
    fetch = [pltpu.make_async_copy(src, at, sem.at[i]) for i, (src, at, dst) in enumerate(stops)]
    store = [pltpu.make_async_copy(at, dst, sem.at[3 + i]) for i, (src, at, dst) in enumerate(stops)]
    for copy in fetch:
        copy.start()
    for i in (1, 2, 0):
        fetch[i].wait()
        store[i].start()
    for copy in store:
        copy.wait()


def solution(mesh):
    n, z = mesh.shape["surf"], mesh.shape["probe"]

    def body(probes, sigma, prior_patch, owner_map, block_perm, col_counts, coef, obs_weight, column_op):
        width, nodes = probes.shape
        blocks, vol = coef.shape
        patch = prior_patch.shape[0]
        cols = obs_weight.shape[1]
        groups = nodes // patch
        depth = blocks // n
        vmem = pl.BlockSpec(memory_space=pltpu.VMEM)
        hbm = pl.BlockSpec(memory_space=pl.ANY)
        hess, diag, quad = pl.pallas_call(
            functools.partial(kernel, n, z, width * z),
            out_shape=(
                jax.ShapeDtypeStruct((width, nodes), F32),
                jax.ShapeDtypeStruct((groups, patch), F32),
                jax.ShapeDtypeStruct((1, width), F32),
            ),
            in_specs=[pl.BlockSpec(memory_space=pltpu.HBM)] * 9,
            out_specs=(vmem, vmem, vmem),
            scratch_shapes=[
                pltpu.VMEM((1, blocks), jnp.int32),
                pltpu.VMEM((1, blocks), jnp.int32),
                pltpu.VMEM((1, blocks), jnp.int32),
                pltpu.VMEM((cols, blocks), BF16),
                pltpu.VMEM((patch, patch), BF16),
                pltpu.VMEM((groups, patch), F32),
                pltpu.VMEM((width, nodes), BF16),
                pltpu.VMEM((vol, vol), BF16),
                pltpu.VMEM((blocks, vol + patch), BF16),
                pltpu.VMEM((n, 1, blocks), jnp.int32),
                pltpu.VMEM((n, 1, blocks), jnp.int32),
                pltpu.VMEM((n, depth, vol + patch), BF16),
                pltpu.VMEM((n, depth, vol + patch), BF16),
                pltpu.VMEM((blocks, vol), F32),
                pltpu.VMEM((blocks, patch), F32),
                pltpu.VMEM((groups, width, patch), F32),
                pltpu.VMEM((blocks * width // CHUNKS, vol), F32),
                pltpu.VMEM((z, groups, patch), F32),
                pltpu.VMEM((n, width, patch), F32),
                pltpu.SemaphoreType.DMA((9,)),
                pltpu.SemaphoreType.DMA((n,)),
                pltpu.SemaphoreType.DMA((n,)),
                pltpu.SemaphoreType.DMA((n,)),
                pltpu.SemaphoreType.DMA((n,)),
                pltpu.SemaphoreType.DMA((CHUNKS, z)),
                pltpu.SemaphoreType.DMA((CHUNKS, z)),
                pltpu.SemaphoreType.DMA((n,)),
                pltpu.SemaphoreType.DMA((n,)),
            ],
            compiler_params=pltpu.CompilerParams(collective_id=0, has_side_effects=True),
        )(
            owner_map.reshape(1, blocks),
            block_perm.reshape(1, blocks),
            col_counts.reshape(1, blocks),
            obs_weight.T,
            prior_patch,
            sigma.reshape(groups, patch),
            probes,
            coef,
            column_op,
        )
        results = (hess, diag, quad)
        hess, diag, quad = pl.pallas_call(
            settle,
            out_shape=tuple(jax.ShapeDtypeStruct(r.shape, r.dtype) for r in results),
            in_specs=[hbm] * 3,
            out_specs=(hbm,) * 3,
            scratch_shapes=[pltpu.VMEM(r.shape, r.dtype) for r in results] + [pltpu.SemaphoreType.DMA((6,))],
        )(*results)
        return hess, diag.reshape(nodes), quad.reshape(width)

    in_specs = (
        P("probe", "surf"),
        P("surf"),
        P(),
        P("surf"),
        P("surf"),
        P("surf"),
        P("surf", None),
        P("surf", None),
        P(),
    )
    out_specs = (P("probe", "surf"), P("surf"), P("probe"))
    return jax.shard_map(body, mesh=mesh, in_specs=in_specs, out_specs=out_specs, check_vma=False)
```

profile of v0, /device:TPU:0, one launch (start us, length us, event | category | flops | bytes accessed | tf_op | source)
XLA Modules:
  0.0 26.3 jit_solution(11294309294027279309)
XLA Ops:
  0.6 23.9 %shard_map.112 = (f32[8,8192]{1,0:T(8,128)}, f32[64,128]{1,0:T(8,128)}, f32[1,8]{1,0:T(1,128)}) custom-call(s32[1,128]{1,0:T(1,128)} %bitcast.9, s32[1,128]{1,0:T(1,128)} %bitcast.10, s32[1,128]{1,0:T(1,128)} %bitcast.11, bf16[64,128]{1,0:T(8,128)(2,1)} %bitcast.8, bf16[128,128]{1,0:T(8,128)(2,1)} %patch_hbm.1, f32[64,128]{1,0:T(8,128)} %bitcast.7, ...), custom_call_target="tpu_custom_call" | custom-call | tf_op jit(solution)/shard_map/pallas_call | solution.py:270
  24.6 1.7 %shard_map.113 = (f32[8,8192]{1,0:T(8,128)}, f32[64,128]{1,0:T(8,128)}, f32[1,8]{1,0:T(1,128)}) custom-call(f32[8,8192]{1,0:T(8,128)} %get-tuple-element.9.hess_in, f32[64,128]{1,0:T(8,128)} %get-tuple-element.10.diag_in, f32[1,8]{1,0:T(1,128)} %get-tuple-element.11.quad_in), custom_call_target="tpu_custom_call" | custom-call | tf_op jit(solution)/shard_map/pallas_call | solution.py:322
where the time goes:
time: 26.4 us; the launch traced here: 26.3 us
  Pallas kernels  25.6 us (97%)
  between operations  0.64 us (2%)
    pallas_call x1, Pallas kernels, body(): pl.pallas_call(functools.partial(kernel, n, z, width * z), out_shape=(jax...  23.9 us
    pallas_call x1, Pallas kernels, body(): pl.pallas_call(settle, out_shape=tuple((jax.ShapeDtypeStruct(r.shape, r.d...  1.71 us

commit v1 on v0

--- a/solution.py
+++ b/solution.py
@@ -242,15 +242,11 @@
     each(1, n, lambda i: quad_copy(i).wait_send())
 
 
-def settle(hess_in, diag_in, quad_in, hess_out, diag_out, quad_out, hess_at, diag_at, quad_at, sem):
-    stops = ((hess_in, hess_at, hess_out), (diag_in, diag_at, diag_out), (quad_in, quad_at, quad_out))
-    fetch = [pltpu.make_async_copy(src, at, sem.at[i]) for i, (src, at, dst) in enumerate(stops)]
-    store = [pltpu.make_async_copy(at, dst, sem.at[3 + i]) for i, (src, at, dst) in enumerate(stops)]
-    for copy in fetch:
+def settle(hess_in, diag_in, quad_in, hess_out, diag_out, quad_out, sem):
+    stops = ((hess_in, hess_out), (diag_in, diag_out), (quad_in, quad_out))
+    store = [pltpu.make_async_copy(src, dst, sem.at[i]) for i, (src, dst) in enumerate(stops)]
+    for copy in store:
         copy.start()
-    for i in (1, 2, 0):
-        fetch[i].wait()
-        store[i].start()
     for copy in store:
         copy.wait()
 
@@ -270,9 +266,9 @@
         hess, diag, quad = pl.pallas_call(
             functools.partial(kernel, n, z, width * z),
             out_shape=(
-                jax.ShapeDtypeStruct((width, nodes), F32),
-                jax.ShapeDtypeStruct((groups, patch), F32),
-                jax.ShapeDtypeStruct((1, width), F32),
+                pltpu.VMEM((width, nodes), F32),
+                pltpu.VMEM((groups, patch), F32),
+                pltpu.VMEM((1, width), F32),
             ),
             in_specs=[pl.BlockSpec(memory_space=pltpu.HBM)] * 9,
             out_specs=(vmem, vmem, vmem),
@@ -306,8 +302,8 @@
                 pltpu.SemaphoreType.DMA((n,)),
                 pltpu.SemaphoreType.DMA((n,)),
             ],
-            compiler_params=pltpu.CompilerParams(collective_id=0, has_side_effects=True),
-        )(
+            compiler_params=pltpu.CompilerParams(collective_id=0, has_side_effects=True, vmem_limit_bytes=32*1024*1024),
+        )(*[pltpu.with_memory_space_constraint(x, pltpu.HBM) for x in (
             owner_map.reshape(1, blocks),
             block_perm.reshape(1, blocks),
             col_counts.reshape(1, blocks),
@@ -317,14 +313,15 @@
             probes,
             coef,
             column_op,
-        )
+        )])
         results = (hess, diag, quad)
         hess, diag, quad = pl.pallas_call(
             settle,
             out_shape=tuple(jax.ShapeDtypeStruct(r.shape, r.dtype) for r in results),
-            in_specs=[hbm] * 3,
+            in_specs=[vmem] * 3,
             out_specs=(hbm,) * 3,
-            scratch_shapes=[pltpu.VMEM(r.shape, r.dtype) for r in results] + [pltpu.SemaphoreType.DMA((6,))],
+            scratch_shapes=[pltpu.SemaphoreType.DMA((3,))],
+            compiler_params=pltpu.CompilerParams(vmem_limit_bytes=1024*1024),
         )(*results)
         return hess, diag.reshape(nodes), quad.reshape(width)
 

time: 26.4 us -> 24.8 us (0.939)
  Pallas kernels: 25.6 us -> 24 us
    pallas_call x1, Pallas kernels: 1.71 us -> 0.74 us  [body(): pl.pallas_call(settle, out_shape=tuple((jax.ShapeDtypeStruct(r.shape, r.d...]
    pallas_call x1, Pallas kernels: 23.9 us -> 23.2 us  [body(): pl.pallas_call(functools.partial(kernel, n, z, width * z), out_shape=(plt...]
where the time goes in v1:
time: 24.8 us; the launch traced here: 24.6 us
  Pallas kernels  24 us (97%)
  between operations  0.64 us (3%)
    pallas_call x1, Pallas kernels, body(): pl.pallas_call(functools.partial(kernel, n, z, width * z), out_shape=(plt...  23.2 us
    pallas_call x1, Pallas kernels, body(): pl.pallas_call(settle, out_shape=tuple((jax.ShapeDtypeStruct(r.shape, r.d...  0.74 us

profile of v1, /device:TPU:0, one launch (start us, length us, event | category | flops | bytes accessed | tf_op | source)
XLA Modules:
  0.0 24.6 jit_solution(7015254977907704644)
XLA Ops:
  0.6 23.2 %shard_map.112 = (f32[8,8192]{1,0:T(8,128)S(1)}, f32[64,128]{1,0:T(8,128)S(1)}, f32[1,8]{1,0:T(1,128)S(1)}) custom-call(s32[1,128]{1,0:T(1,128)} %bitcast.9, s32[1,128]{1,0:T(1,128)} %bitcast.10, s32[1,128]{1,0:T(1,128)} %bitcast.11, bf16[64,128]{1,0:T(8,128)(2,1)} %bitcast.8, bf16[128,128]{1,0:T(8,128)(2,1)} %patch_hbm.1, f32[64,128]{1,0:T(8,128)} %bitcast.7, ...), custom_call_target="tpu_custom_call" | custom-call | tf_op jit(solution)/shard_map/pallas_call | solution.py:266
  23.9 0.7 %shard_map.113 = (f32[8,8192]{1,0:T(8,128)}, f32[64,128]{1,0:T(8,128)}, f32[1,8]{1,0:T(1,128)}) custom-call(f32[8,8192]{1,0:T(8,128)S(1)} %get-tuple-element.9.hess_in, f32[64,128]{1,0:T(8,128)S(1)} %get-tuple-element.10.diag_in, f32[1,8]{1,0:T(1,128)S(1)} %get-tuple-element.11.quad_in), custom_call_target="tpu_custom_call" | custom-call | tf_op jit(solution)/shard_map/pallas_call | solution.py:318

commit v2 on v1

v2 whole, which is shorter than its diff:
```python
import functools

import jax
import jax.numpy as jnp
from jax import lax
from jax.experimental import pallas as pl
from jax.experimental.pallas import tpu as pltpu
from jax.sharding import PartitionSpec as P

F32 = jnp.float32
BF16 = jnp.bfloat16
NT = (((1,), (1,)), ((), ()))
PARTS = 4


def kernel(
    n, z, total_probes,
    owner_hbm, slot_hbm, count_hbm, obs_hbm, patch_hbm, sigma_hbm, probes_hbm, coef_hbm, op_hbm,
    hess_ref, diag_ref, quad_ref,
    owner_ref, slot_ref, count_ref, obs_ref, patch_ref, sigma_ref, probes_ref,
    op_ref, ext_ref, ask_out, ask_in, row_out, row_in, value_ref, spread_ref, field_ref, sens_ref, hold_ref,
    diag_in, quad_in,
    load_sem, ask_send, ask_recv, row_send, row_recv, diag_send, diag_recv, quad_send, quad_recv,
):
    width, nodes = probes_ref.shape
    blocks, vol = coef_hbm.shape
    cols = obs_ref.shape[0]
    patch = patch_ref.shape[0]
    groups = nodes // patch
    depth = blocks // n
    tiles = vol // patch
    me = lax.axis_index("surf")
    zme = lax.axis_index("probe")
    barrier = pltpu.get_barrier_semaphore()
    paired = n & (n - 1) == 0

    def flip(i):
        out, bit = 0, 1
        while bit < n:
            out = out + lax.rem(lax.div(me, bit) + lax.div(jnp.int32(i), jnp.int32(bit)), 2) * bit
            bit *= 2
        return out

    def peer_to(i):
        return flip(i) if paired else lax.rem(me + i, n)

    def peer_from(i):
        return flip(i) if paired else lax.rem(me + n - i, n)

    def probe_peer(i):
        return lax.rem(zme + i, z)

    def each(lo, hi, f):
        def step(i, c):
            f(i)
            return c

        lax.fori_loop(lo, hi, step, 0)

    def greet(i):
        pl.semaphore_signal(barrier, inc=1, device_id={"surf": peer_to(n - i)}, device_id_type=pl.DeviceIdType.MESH)

    def greet_z(i):
        pl.semaphore_signal(barrier, inc=1, device_id={"probe": probe_peer(i)}, device_id_type=pl.DeviceIdType.MESH)

    each(1, z, greet_z)
    each(1, n, greet)

    smalls = (
        (owner_hbm, owner_ref), (slot_hbm, slot_ref), (count_hbm, count_ref), (obs_hbm, obs_ref),
        (patch_hbm, patch_ref), (sigma_hbm, sigma_ref), (probes_hbm, probes_ref),
    )
    loads = [pltpu.make_async_copy(src, dst, load_sem.at[i]) for i, (src, dst) in enumerate(smalls)]
    load_coef = pltpu.make_async_copy(coef_hbm, ext_ref.at[:, pl.ds(0, vol)], load_sem.at[7])
    load_op = pltpu.make_async_copy(op_hbm, op_ref, load_sem.at[8])
    for load in loads + [load_coef, load_op]:
        load.start()
    for load in loads[:2]:
        load.wait()

    square = (blocks, blocks)
    down = lax.broadcasted_iota(jnp.int32, square, 0)
    across = lax.broadcasted_iota(jnp.int32, square, 1)
    owner = jnp.broadcast_to(owner_ref[...], square).astype(F32)
    same = (owner == jnp.transpose(owner)) & (down < across)
    rank = jnp.sum(jnp.where(same, 1.0, 0.0), axis=0, keepdims=True)
    key = owner * depth + rank
    turn = lax.div(down, depth)
    if paired:
        turn = jnp.bitwise_xor(turn, me)
    else:
        turn = lax.rem(turn + me, n)
    chosen = key == (turn * depth + lax.rem(down, depth)).astype(F32)
    slots = jnp.broadcast_to(slot_ref[...], square).astype(F32)
    asked = jnp.sum(jnp.where(chosen, slots, 0.0), axis=1, keepdims=True)
    asked = jnp.where(across == down, jnp.broadcast_to(asked, square), 0.0).astype(jnp.int32)
    ask_out[...] = jnp.sum(asked.reshape(n, depth, blocks), axis=1, keepdims=True)

    pl.semaphore_wait(barrier, (n - 1) + (z - 1))

    def ask(i):
        return pltpu.make_async_remote_copy(
            src_ref=ask_out.at[i],
            dst_ref=ask_in.at[i],
            send_sem=ask_send.at[i],
            recv_sem=ask_recv.at[i],
            device_id={"surf": peer_to(i)},
            device_id_type=pl.DeviceIdType.MESH,
        )

    def row(i):
        return pltpu.make_async_remote_copy(
            src_ref=row_out.at[i],
            dst_ref=row_in.at[i],
            send_sem=row_send.at[i],
            recv_sem=row_recv.at[i],
            device_id={"surf": peer_from(i)},
            device_id_type=pl.DeviceIdType.MESH,
        )

    def quad_copy(i):
        return pltpu.make_async_remote_copy(
            src_ref=quad_in.at[me],
            dst_ref=quad_in.at[me],
            send_sem=quad_send.at[i],
            recv_sem=quad_recv.at[i],
            device_id={"surf": peer_to(i)},
            device_id_type=pl.DeviceIdType.MESH,
        )

    def diag_copy(i):
        return pltpu.make_async_remote_copy(
            src_ref=diag_in.at[zme],
            dst_ref=diag_in.at[zme],
            send_sem=diag_send.at[i],
            recv_sem=diag_recv.at[i],
            device_id={"probe": probe_peer(i)},
            device_id_type=pl.DeviceIdType.MESH,
        )

    each(1, n, lambda i: ask(n - i).start())

    for load in loads[2:4]:
        load.wait()
    lane = lax.rem(across, patch)
    block = jnp.sum(jnp.where(chosen, across.astype(F32), 0.0), axis=1, keepdims=True)
    spot = (2 * lax.rem(across, groups) + lax.div(across, groups)).astype(F32)
    place = jnp.where(jnp.broadcast_to(block, square) == spot, 1.0, 0.0)
    gather = place.astype(BF16)
    scatter = jnp.transpose(place).astype(BF16)
    counts = jnp.broadcast_to(count_ref[...], square).astype(F32)
    counts = jnp.sum(jnp.where(chosen, counts, 0.0), axis=1, keepdims=True)
    keep_lane = lax.rem(lax.broadcasted_iota(jnp.int32, (blocks, patch), 1), cols).astype(F32)
    keep = jnp.where(keep_lane < counts, 1.0, 0.0)
    twice = (
        lax.rem(lax.broadcasted_iota(jnp.int32, (cols, patch), 1), cols)
        == lax.broadcasted_iota(jnp.int32, (cols, patch), 0)
    ).astype(F32).astype(BF16)
    ext_ref[:, vol:] = lax.dot_general(
        obs_ref[...], twice, (((0,), (0,)), ((), ())), preferred_element_type=F32
    ).astype(BF16)

    for load in loads[4:]:
        load.wait()
    values = probes_ref[...].astype(F32)
    stacked = jnp.concatenate([values[:, k * patch:(k + 1) * patch] for k in range(groups)], axis=0)
    value_ref[...] = stacked
    mixed = jnp.dot(stacked.astype(BF16), patch_ref[...], preferred_element_type=F32)
    for k in range(groups):
        spread_ref[k * width:(k + 1) * width, :] = (
            (mixed[k * width:(k + 1) * width] * sigma_ref[k:k + 1, :]).astype(BF16).astype(F32)
        )
    low = lax.broadcasted_iota(jnp.int32, (groups, patch), 1) < cols
    halves = []
    for p in range(width):
        field = spread_ref[pl.ds(p, groups, stride=width), :]
        turned = pltpu.roll(field, cols, 1)
        halves.append(jnp.concatenate([jnp.where(low, field, turned), jnp.where(low, turned, field)], axis=0).astype(BF16))
    ordered = jnp.dot(gather, jnp.concatenate(halves, axis=1), preferred_element_type=F32)
    for p in range(width):
        field_ref[p] = (ordered[:, p * patch:(p + 1) * patch] * keep).astype(BF16)

    load_coef.wait()

    def serve(lo, hi):
        each(max(lo, 1), hi, lambda i: ask(i).wait_recv())
        rows_of = (hi - lo) * depth
        shape = (rows_of, blocks)
        wanted = jnp.sum(ask_in[lo:hi], axis=0)
        if lo == 0:
            wanted = wanted + ask_out[0]
        here = lax.broadcasted_iota(jnp.int32, shape, 1)
        diagonal = here == lax.broadcasted_iota(jnp.int32, shape, 0) + lo * depth
        wanted = jnp.sum(jnp.where(diagonal, jnp.broadcast_to(wanted, shape).astype(F32), 0.0), axis=1, keepdims=True)
        pick = jnp.where(jnp.broadcast_to(wanted, shape) == here.astype(F32), 1.0, 0.0).astype(BF16)
        rows = jnp.dot(pick, ext_ref[...], preferred_element_type=F32).astype(BF16)
        row_out[lo:hi] = rows.reshape(hi - lo, depth, rows.shape[1])
        if lo == 0:
            row_in[0] = row_out[0]
        each(max(lo, 1), hi, lambda i: row(i).start())

    step = n // PARTS
    ask_in[0] = jnp.zeros(ask_in.shape[1:], jnp.int32)
    serve(0, step)
    serve(step, (PARTS - 1) * step)
    serve((PARTS - 1) * step, n)
    load_op.wait()

    rows_of = blocks // PARTS
    for g in range(PARTS):
        each(max(g * step, 1), (g + 1) * step, lambda i: row(i).wait_recv())
        span = slice(g * rows_of, (g + 1) * rows_of)
        got = row_in[g * step:(g + 1) * step].reshape(rows_of, row_in.shape[2])
        coef = got[:, :vol]
        weight = got[:, vol:].astype(F32)
        lifted = jnp.concatenate(
            [jnp.concatenate([field_ref[p, span, :]] * tiles, axis=1) * coef for p in range(width)], axis=0
        )
        state = jnp.dot(lifted, op_ref[...], preferred_element_type=F32)
        weight = jnp.concatenate([weight] * tiles, axis=1)
        weighted = jnp.concatenate(
            [(state[p * rows_of:(p + 1) * rows_of] * weight).astype(BF16) for p in range(width)], axis=0
        )
        adjoint = lax.dot_general(weighted, op_ref[...], NT, preferred_element_type=F32)
        coef = coef.astype(F32)
        for p in range(width):
            at = slice(p * rows_of, (p + 1) * rows_of)
            total = None
            for t in range(tiles):
                cut = slice(t * patch, (t + 1) * patch)
                term = adjoint[at, cut] * coef[:, cut]
                total = term if total is None else total + term
            total = (total + pltpu.roll(total, cols, 1)) * keep[span]
            sens_ref[span, p * patch:(p + 1) * patch] = total.astype(BF16)

    split = jnp.dot(scatter, sens_ref[...], preferred_element_type=F32)
    scaled = []
    for p in range(width):
        cut = slice(p * patch, (p + 1) * patch)
        scaled.append((jnp.where(low, split[:groups, cut], split[groups:, cut]) * sigma_ref[...]).astype(BF16))
    back = lax.dot_general(jnp.concatenate(scaled, axis=0), patch_ref[...], NT, preferred_element_type=F32)
    total = None
    energy = []
    for p in range(width):
        term = back[p * groups:(p + 1) * groups]
        value = value_ref[pl.ds(p, groups, stride=width), :]
        product = value * term
        total = product if total is None else total + product
        energy.append(jnp.sum(product, axis=0, keepdims=True))
        hold_ref[pl.ds(p, groups, stride=width), :] = value + term
    diag_in[zme] = total.astype(BF16)
    each(1, z, lambda i: diag_copy(i).start())
    quad_in[me] = jnp.concatenate(energy, axis=0)
    each(1, n, lambda i: quad_copy(n - i).start())
    for k in range(groups):
        hess_ref[:, k * patch:(k + 1) * patch] = hold_ref[k * width:(k + 1) * width, :]
    each(1, n, lambda i: ask(i).wait_send())
    each(1, n, lambda i: row(i).wait_send())
    each(1, n, lambda i: quad_copy(i).wait_recv())
    energy = lax.fori_loop(1, n, lambda i, s: s + quad_in[i], quad_in[0])
    energy = jnp.broadcast_to(jnp.sum(energy, axis=1, keepdims=True), (width, patch))
    diagonal = lax.broadcasted_iota(jnp.int32, (width, patch), 0) == lax.broadcasted_iota(jnp.int32, (width, patch), 1)
    quad_ref[...] = jnp.sum(jnp.where(diagonal, energy, 0.0), axis=0, keepdims=True)[:, :width]
    each(1, n, lambda i: quad_copy(i).wait_send())
    each(1, z, lambda i: diag_copy(i).wait_send())
    each(1, z, lambda i: diag_copy(i).wait_recv())
    total = diag_in[0].astype(F32)
    for i in range(1, z):
        total = total + diag_in[i].astype(F32)
    diag_ref[...] = total * (1.0 / total_probes)


def settle(hess_in, diag_in, quad_in, hess_out, diag_out, quad_out, sem):
    stops = ((hess_in, hess_out), (diag_in, diag_out), (quad_in, quad_out))
    store = [pltpu.make_async_copy(src, dst, sem.at[i]) for i, (src, dst) in enumerate(stops)]
    for copy in store:
        copy.start()
    for copy in store:
        copy.wait()


def solution(mesh):
    n, z = mesh.shape["surf"], mesh.shape["probe"]

    def body(probes, sigma, prior_patch, owner_map, block_perm, col_counts, coef, obs_weight, column_op):
        width, nodes = probes.shape
        blocks, vol = coef.shape
        patch = prior_patch.shape[0]
        cols = obs_weight.shape[1]
        groups = nodes // patch
        depth = blocks // n
        vmem = pl.BlockSpec(memory_space=pltpu.VMEM)
        hbm = pl.BlockSpec(memory_space=pl.ANY)
        operands = (
            owner_map.reshape(1, blocks),
            block_perm.reshape(1, blocks),
            col_counts.reshape(1, blocks),
            obs_weight.T,
            prior_patch,
            sigma.reshape(groups, patch),
            probes,
            coef,
            column_op,
        )
        results = pl.pallas_call(
            functools.partial(kernel, n, z, width * z),
            out_shape=(
                pltpu.VMEM((width, nodes), F32),
                pltpu.VMEM((groups, patch), F32),
                pltpu.VMEM((1, width), F32),
            ),
            in_specs=[pl.BlockSpec(memory_space=pltpu.HBM)] * 9,
            out_specs=(vmem, vmem, vmem),
            scratch_shapes=[
                pltpu.VMEM((1, blocks), jnp.int32),
                pltpu.VMEM((1, blocks), jnp.int32),
                pltpu.VMEM((1, blocks), jnp.int32),
                pltpu.VMEM((cols, blocks), BF16),
                pltpu.VMEM((patch, patch), BF16),
                pltpu.VMEM((groups, patch), F32),
                pltpu.VMEM((width, nodes), BF16),
                pltpu.VMEM((vol, vol), BF16),
                pltpu.VMEM((blocks, vol + patch), BF16),
                pltpu.VMEM((n, 1, blocks), jnp.int32),
                pltpu.VMEM((n, 1, blocks), jnp.int32),
                pltpu.VMEM((n, depth, vol + patch), BF16),
                pltpu.VMEM((n, depth, vol + patch), BF16),
                pltpu.VMEM((groups * width, patch), F32),
                pltpu.VMEM((groups * width, patch), F32),
                pltpu.VMEM((width, blocks, patch), BF16),
                pltpu.VMEM((blocks, width * patch), BF16),
                pltpu.VMEM((groups * width, patch), F32),
                pltpu.VMEM((z, groups, patch), BF16),
                pltpu.VMEM((n, width, patch), F32),
                pltpu.SemaphoreType.DMA((9,)),
                pltpu.SemaphoreType.DMA((n,)),
                pltpu.SemaphoreType.DMA((n,)),
                pltpu.SemaphoreType.DMA((n,)),
                pltpu.SemaphoreType.DMA((n,)),
                pltpu.SemaphoreType.DMA((z,)),
                pltpu.SemaphoreType.DMA((z,)),
                pltpu.SemaphoreType.DMA((n,)),
                pltpu.SemaphoreType.DMA((n,)),
            ],
            compiler_params=pltpu.CompilerParams(
                collective_id=0, has_side_effects=True, vmem_limit_bytes=32 * 1024 * 1024
            ),
        )(*[pltpu.with_memory_space_constraint(x, pltpu.HBM) for x in operands])
        hess, diag, quad = pl.pallas_call(
            settle,
            out_shape=tuple(jax.ShapeDtypeStruct(r.shape, r.dtype) for r in results),
            in_specs=[vmem] * 3,
            out_specs=(hbm,) * 3,
            scratch_shapes=[pltpu.SemaphoreType.DMA((3,))],
            compiler_params=pltpu.CompilerParams(vmem_limit_bytes=1024 * 1024),
        )(*results)
        return hess, diag.reshape(nodes), quad.reshape(width)

    in_specs = (
        P("probe", "surf"),
        P("surf"),
        P(),
        P("surf"),
        P("surf"),
        P("surf"),
        P("surf", None),
        P("surf", None),
        P(),
    )
    out_specs = (P("probe", "surf"), P("surf"), P("probe"))
    return jax.shard_map(body, mesh=mesh, in_specs=in_specs, out_specs=out_specs, check_vma=False)
```

time: 24.8 us -> 22.1 us (0.89)
  Pallas kernels: 24 us -> 21.3 us
    pallas_call x1, Pallas kernels: 23.2 us -> 20.6 us  [body(): pl.pallas_call(functools.partial(kernel, n, z, width * z), out_shape=(plt...]
where the time goes in v2:
time: 22.1 us; the launch traced here: 22 us
  Pallas kernels  21.3 us (96%)
  between operations  0.64 us (3%)
    pallas_call x1, Pallas kernels, body(): pl.pallas_call(functools.partial(kernel, n, z, width * z), out_shape=(plt...  20.6 us
    pallas_call x1, Pallas kernels, body(): pl.pallas_call(settle, out_shape=tuple((jax.ShapeDtypeStruct(r.shape, r.d...  0.74 us

profile of v2, /device:TPU:0, one launch (start us, length us, event | category | flops | bytes accessed | tf_op | source)
XLA Modules:
  0.0 22.0 jit_solution(18144529051715335875)
XLA Ops:
  0.6 20.6 %shard_map.112 = (f32[8,8192]{1,0:T(8,128)S(1)}, f32[64,128]{1,0:T(8,128)S(1)}, f32[1,8]{1,0:T(1,128)S(1)}) custom-call(s32[1,128]{1,0:T(1,128)} %bitcast.9, s32[1,128]{1,0:T(1,128)} %bitcast.10, s32[1,128]{1,0:T(1,128)} %bitcast.11, bf16[64,128]{1,0:T(8,128)(2,1)} %bitcast.8, bf16[128,128]{1,0:T(8,128)(2,1)} %patch_hbm.1, f32[64,128]{1,0:T(8,128)} %bitcast.7, ...), custom_call_target="tpu_custom_call" | custom-call | tf_op jit(solution)/shard_map/pallas_call | solution.py:305
  21.2 0.7 %shard_map.113 = (f32[8,8192]{1,0:T(8,128)}, f32[64,128]{1,0:T(8,128)}, f32[1,8]{1,0:T(1,128)}) custom-call(f32[8,8192]{1,0:T(8,128)S(1)} %get-tuple-element.9.hess_in, f32[64,128]{1,0:T(8,128)S(1)} %get-tuple-element.10.diag_in, f32[1,8]{1,0:T(1,128)S(1)} %get-tuple-element.11.quad_in), custom_call_target="tpu_custom_call" | custom-call | tf_op jit(solution)/shard_map/pallas_call | solution.py:349

commit v3 on v2

--- a/solution.py
+++ b/solution.py
@@ -11,16 +11,18 @@
 BF16 = jnp.bfloat16
 NT = (((1,), (1,)), ((), ()))
 PARTS = 4
+CHUNKS = ((0, 1), (1, 2), (2, 4))
 
 
 def kernel(
     n, z, total_probes,
     owner_hbm, slot_hbm, count_hbm, obs_hbm, patch_hbm, sigma_hbm, probes_hbm, coef_hbm, op_hbm,
     hess_ref, diag_ref, quad_ref,
-    owner_ref, slot_ref, count_ref, obs_ref, patch_ref, sigma_ref, probes_ref,
+    index_ref, obs_ref, patch_ref, sigma_ref, probes_ref,
     op_ref, ext_ref, ask_out, ask_in, row_out, row_in, value_ref, spread_ref, field_ref, sens_ref, hold_ref,
     diag_in, quad_in,
     load_sem, ask_send, ask_recv, row_send, row_recv, diag_send, diag_recv, quad_send, quad_recv,
+    answer,
 ):
     width, nodes = probes_ref.shape
     blocks, vol = coef_hbm.shape
@@ -34,11 +36,25 @@
     barrier = pltpu.get_barrier_semaphore()
     paired = n & (n - 1) == 0
 
+    signs = []
+    if paired:
+        bit = 1
+        while bit < n:
+            signs.append((1 - 2 * lax.rem(lax.div(me, bit), 2)) * bit)
+            bit *= 2
+
+    def code(i):
+        return (0, 1, 2, 4, 3, 5, 6, 7)[i] if n == 8 else i
+
     def flip(i):
-        out, bit = 0, 1
-        while bit < n:
-            out = out + lax.rem(lax.div(me, bit) + lax.div(jnp.int32(i), jnp.int32(bit)), 2) * bit
-            bit *= 2
+        out = me
+        if isinstance(i, int):
+            for b, sign in enumerate(signs):
+                if code(i) >> b & 1:
+                    out = out + sign
+        else:
+            for b, sign in enumerate(signs):
+                out = out + sign * lax.rem(lax.div(i, jnp.int32(1 << b)), 2)
         return out
 
     def peer_to(i):
@@ -51,69 +67,76 @@
         return lax.rem(zme + i, z)
 
     def each(lo, hi, f):
-        def step(i, c):
-            f(i)
-            return c
-
-        lax.fori_loop(lo, hi, step, 0)
+        if hi - lo <= 8:
+            for i in range(lo, hi):
+                f(i)
+        else:
+            lax.fori_loop(lo, hi, lambda i, c: (f(i), c)[1], 0)
 
     def greet(i):
         pl.semaphore_signal(barrier, inc=1, device_id={"surf": peer_to(n - i)}, device_id_type=pl.DeviceIdType.MESH)
 
-    def greet_z(i):
-        pl.semaphore_signal(barrier, inc=1, device_id={"probe": probe_peer(i)}, device_id_type=pl.DeviceIdType.MESH)
-
-    each(1, z, greet_z)
+    def tell(sem, lo, hi):
+        def step(i, c):
+            pl.semaphore_signal(sem, inc=1, device_id={"probe": i}, device_id_type=pl.DeviceIdType.MESH)
+            return c
+
+        lax.fori_loop(lo, hi, step, 0)
+
+    def settled(ref, sem):
+        pltpu.make_async_copy(ref, ref, sem).wait()
+
+    for i, src in enumerate((owner_hbm, slot_hbm)):
+        pltpu.make_async_copy(src, index_ref.at[i], load_sem.at[0]).start()
     each(1, n, greet)
-
-    smalls = (
-        (owner_hbm, owner_ref), (slot_hbm, slot_ref), (count_hbm, count_ref), (obs_hbm, obs_ref),
-        (patch_hbm, patch_ref), (sigma_hbm, sigma_ref), (probes_hbm, probes_ref),
-    )
-    loads = [pltpu.make_async_copy(src, dst, load_sem.at[i]) for i, (src, dst) in enumerate(smalls)]
-    load_coef = pltpu.make_async_copy(coef_hbm, ext_ref.at[:, pl.ds(0, vol)], load_sem.at[7])
-    load_op = pltpu.make_async_copy(op_hbm, op_ref, load_sem.at[8])
+    tell(barrier, zme + 1, z)
+
+    smalls = ((count_hbm, index_ref.at[2]), (obs_hbm, obs_ref), (patch_hbm, patch_ref), (sigma_hbm, sigma_ref), (probes_hbm, probes_ref))
+    loads = [pltpu.make_async_copy(src, dst, load_sem.at[1 + i]) for i, (src, dst) in enumerate(smalls)]
+    load_coef = pltpu.make_async_copy(coef_hbm, ext_ref.at[:, pl.ds(0, vol)], load_sem.at[6])
+    load_op = pltpu.make_async_copy(op_hbm, op_ref, load_sem.at[7])
     for load in loads + [load_coef, load_op]:
         load.start()
-    for load in loads[:2]:
-        load.wait()
+    settled(index_ref.at[0:2], load_sem.at[0])
 
     square = (blocks, blocks)
     down = lax.broadcasted_iota(jnp.int32, square, 0)
     across = lax.broadcasted_iota(jnp.int32, square, 1)
-    owner = jnp.broadcast_to(owner_ref[...], square).astype(F32)
+    owner = jnp.broadcast_to(index_ref[0], square).astype(F32)
     same = (owner == jnp.transpose(owner)) & (down < across)
     rank = jnp.sum(jnp.where(same, 1.0, 0.0), axis=0, keepdims=True)
     key = owner * depth + rank
     turn = lax.div(down, depth)
+    if n == 8:
+        turn = jnp.where(turn == 3, 4, jnp.where(turn == 4, 3, turn))
     if paired:
         turn = jnp.bitwise_xor(turn, me)
     else:
         turn = lax.rem(turn + me, n)
     chosen = key == (turn * depth + lax.rem(down, depth)).astype(F32)
-    slots = jnp.broadcast_to(slot_ref[...], square).astype(F32)
+    slots = jnp.broadcast_to(index_ref[1], square).astype(F32)
     asked = jnp.sum(jnp.where(chosen, slots, 0.0), axis=1, keepdims=True)
     asked = jnp.where(across == down, jnp.broadcast_to(asked, square), 0.0).astype(jnp.int32)
     ask_out[...] = jnp.sum(asked.reshape(n, depth, blocks), axis=1, keepdims=True)
 
-    pl.semaphore_wait(barrier, (n - 1) + (z - 1))
-
-    def ask(i):
+    pl.semaphore_wait(barrier, (n - 1) + zme)
+
+    def ask(i, part):
         return pltpu.make_async_remote_copy(
             src_ref=ask_out.at[i],
             dst_ref=ask_in.at[i],
-            send_sem=ask_send.at[i],
-            recv_sem=ask_recv.at[i],
+            send_sem=ask_send,
+            recv_sem=ask_recv.at[part],
             device_id={"surf": peer_to(i)},
             device_id_type=pl.DeviceIdType.MESH,
         )
 
-    def row(i):
+    def row(i, part):
         return pltpu.make_async_remote_copy(
             src_ref=row_out.at[i],
             dst_ref=row_in.at[i],
-            send_sem=row_send.at[i],
-            recv_sem=row_recv.at[i],
+            send_sem=row_send,
+            recv_sem=row_recv.at[part],
             device_id={"surf": peer_from(i)},
             device_id_type=pl.DeviceIdType.MESH,
         )
@@ -122,8 +145,8 @@
         return pltpu.make_async_remote_copy(
             src_ref=quad_in.at[me],
             dst_ref=quad_in.at[me],
-            send_sem=quad_send.at[i],
-            recv_sem=quad_recv.at[i],
+            send_sem=quad_send,
+            recv_sem=quad_recv,
             device_id={"surf": peer_to(i)},
             device_id_type=pl.DeviceIdType.MESH,
         )
@@ -132,15 +155,18 @@
         return pltpu.make_async_remote_copy(
             src_ref=diag_in.at[zme],
             dst_ref=diag_in.at[zme],
-            send_sem=diag_send.at[i],
-            recv_sem=diag_recv.at[i],
+            send_sem=diag_send,
+            recv_sem=diag_recv,
             device_id={"probe": probe_peer(i)},
             device_id_type=pl.DeviceIdType.MESH,
         )
 
-    each(1, n, lambda i: ask(n - i).start())
-
-    for load in loads[2:4]:
+    step = n // PARTS
+    for part in reversed(range(PARTS)):
+        each(max(part * step, 1), (part + 1) * step, lambda i: ask(i, part).start())
+    tell(answer, 0, zme)
+
+    for load in loads[:2]:
         load.wait()
     lane = lax.rem(across, patch)
     block = jnp.sum(jnp.where(chosen, across.astype(F32), 0.0), axis=1, keepdims=True)
@@ -148,7 +174,7 @@
     place = jnp.where(jnp.broadcast_to(block, square) == spot, 1.0, 0.0)
     gather = place.astype(BF16)
     scatter = jnp.transpose(place).astype(BF16)
-    counts = jnp.broadcast_to(count_ref[...], square).astype(F32)
+    counts = jnp.broadcast_to(index_ref[2], square).astype(F32)
     counts = jnp.sum(jnp.where(chosen, counts, 0.0), axis=1, keepdims=True)
     keep_lane = lax.rem(lax.broadcasted_iota(jnp.int32, (blocks, patch), 1), cols).astype(F32)
     keep = jnp.where(keep_lane < counts, 1.0, 0.0)
@@ -160,7 +186,7 @@
         obs_ref[...], twice, (((0,), (0,)), ((), ())), preferred_element_type=F32
     ).astype(BF16)
 
-    for load in loads[4:]:
+    for load in loads[2:]:
         load.wait()
     values = probes_ref[...].astype(F32)
     stacked = jnp.concatenate([values[:, k * patch:(k + 1) * patch] for k in range(groups)], axis=0)
@@ -182,8 +208,10 @@
 
     load_coef.wait()
 
-    def serve(lo, hi):
-        each(max(lo, 1), hi, lambda i: ask(i).wait_recv())
+    def serve(part):
+        lo, hi = part * step, (part + 1) * step
+        if hi > max(lo, 1):
+            settled(ask_in.at[max(lo, 1):hi], ask_recv.at[part])
         rows_of = (hi - lo) * depth
         shape = (rows_of, blocks)
         wanted = jnp.sum(ask_in[lo:hi], axis=0)
@@ -197,20 +225,26 @@
         row_out[lo:hi] = rows.reshape(hi - lo, depth, rows.shape[1])
         if lo == 0:
             row_in[0] = row_out[0]
-        each(max(lo, 1), hi, lambda i: row(i).start())
-
-    step = n // PARTS
+        each(max(lo, 1), hi, lambda i: row(i, part).start())
+
     ask_in[0] = jnp.zeros(ask_in.shape[1:], jnp.int32)
-    serve(0, step)
-    serve(step, (PARTS - 1) * step)
-    serve((PARTS - 1) * step, n)
+    for part in range(PARTS):
+        serve(part)
     load_op.wait()
 
-    rows_of = blocks // PARTS
-    for g in range(PARTS):
-        each(max(g * step, 1), (g + 1) * step, lambda i: row(i).wait_recv())
-        span = slice(g * rows_of, (g + 1) * rows_of)
-        got = row_in[g * step:(g + 1) * step].reshape(rows_of, row_in.shape[2])
+    for first, last in CHUNKS:
+        if last == PARTS:
+
+            @pl.when(zme < z - 1)
+            def _():
+                pl.semaphore_wait(answer, z - 1 - zme)
+
+        for part in range(first, last):
+            if (part + 1) * step > max(part * step, 1):
+                settled(row_in.at[max(part * step, 1):(part + 1) * step], row_recv.at[part])
+        rows_of = (last - first) * step * depth
+        span = slice(first * step * depth, last * step * depth)
+        got = row_in[first * step:last * step].reshape(rows_of, row_in.shape[2])
         coef = got[:, :vol]
         weight = got[:, vol:].astype(F32)
         lifted = jnp.concatenate(
@@ -240,30 +274,31 @@
         scaled.append((jnp.where(low, split[:groups, cut], split[groups:, cut]) * sigma_ref[...]).astype(BF16))
     back = lax.dot_general(jnp.concatenate(scaled, axis=0), patch_ref[...], NT, preferred_element_type=F32)
     total = None
+    for p in range(width):
+        product = value_ref[pl.ds(p, groups, stride=width), :] * back[p * groups:(p + 1) * groups]
+        total = product if total is None else total + product
+    diag_in[zme] = total.astype(BF16)
+    each(1, z, lambda i: diag_copy(i).start())
     energy = []
     for p in range(width):
         term = back[p * groups:(p + 1) * groups]
         value = value_ref[pl.ds(p, groups, stride=width), :]
-        product = value * term
-        total = product if total is None else total + product
-        energy.append(jnp.sum(product, axis=0, keepdims=True))
+        energy.append(jnp.sum(value * term, axis=0, keepdims=True))
         hold_ref[pl.ds(p, groups, stride=width), :] = value + term
-    diag_in[zme] = total.astype(BF16)
-    each(1, z, lambda i: diag_copy(i).start())
     quad_in[me] = jnp.concatenate(energy, axis=0)
     each(1, n, lambda i: quad_copy(n - i).start())
     for k in range(groups):
         hess_ref[:, k * patch:(k + 1) * patch] = hold_ref[k * width:(k + 1) * width, :]
-    each(1, n, lambda i: ask(i).wait_send())
-    each(1, n, lambda i: row(i).wait_send())
-    each(1, n, lambda i: quad_copy(i).wait_recv())
+    settled(ask_out.at[1:n], ask_send)
+    settled(row_out.at[1:n], row_send)
+    settled(quad_in.at[1:n], quad_recv)
     energy = lax.fori_loop(1, n, lambda i, s: s + quad_in[i], quad_in[0])
     energy = jnp.broadcast_to(jnp.sum(energy, axis=1, keepdims=True), (width, patch))
     diagonal = lax.broadcasted_iota(jnp.int32, (width, patch), 0) == lax.broadcasted_iota(jnp.int32, (width, patch), 1)
     quad_ref[...] = jnp.sum(jnp.where(diagonal, energy, 0.0), axis=0, keepdims=True)[:, :width]
-    each(1, n, lambda i: quad_copy(i).wait_send())
-    each(1, z, lambda i: diag_copy(i).wait_send())
-    each(1, z, lambda i: diag_copy(i).wait_recv())
+    settled(quad_in.at[1:n], quad_send)
+    settled(diag_in.at[1:z], diag_send)
+    settled(diag_in.at[1:z], diag_recv)
     total = diag_in[0].astype(F32)
     for i in range(1, z):
         total = total + diag_in[i].astype(F32)
@@ -312,9 +347,7 @@
             in_specs=[pl.BlockSpec(memory_space=pltpu.HBM)] * 9,
             out_specs=(vmem, vmem, vmem),
             scratch_shapes=[
-                pltpu.VMEM((1, blocks), jnp.int32),
-                pltpu.VMEM((1, blocks), jnp.int32),
-                pltpu.VMEM((1, blocks), jnp.int32),
+                pltpu.VMEM((3, 1, blocks), jnp.int32),
                 pltpu.VMEM((cols, blocks), BF16),
                 pltpu.VMEM((patch, patch), BF16),
                 pltpu.VMEM((groups, patch), F32),
@@ -332,15 +365,16 @@
                 pltpu.VMEM((groups * width, patch), F32),
                 pltpu.VMEM((z, groups, patch), BF16),
                 pltpu.VMEM((n, width, patch), F32),
-                pltpu.SemaphoreType.DMA((9,)),
-                pltpu.SemaphoreType.DMA((n,)),
-                pltpu.SemaphoreType.DMA((n,)),
-                pltpu.SemaphoreType.DMA((n,)),
-                pltpu.SemaphoreType.DMA((n,)),
-                pltpu.SemaphoreType.DMA((z,)),
-                pltpu.SemaphoreType.DMA((z,)),
-                pltpu.SemaphoreType.DMA((n,)),
-                pltpu.SemaphoreType.DMA((n,)),
+                pltpu.SemaphoreType.DMA((8,)),
+                pltpu.SemaphoreType.DMA,
+                pltpu.SemaphoreType.DMA((PARTS,)),
+                pltpu.SemaphoreType.DMA,
+                pltpu.SemaphoreType.DMA((PARTS,)),
+                pltpu.SemaphoreType.DMA,
+                pltpu.SemaphoreType.DMA,
+                pltpu.SemaphoreType.DMA,
+                pltpu.SemaphoreType.DMA,
+                pltpu.SemaphoreType.REGULAR,
             ],
             compiler_params=pltpu.CompilerParams(
                 collective_id=0, has_side_effects=True, vmem_limit_bytes=32 * 1024 * 1024

time: 22.1 us -> 21.2 us (0.959)
  Pallas kernels: 21.3 us -> 20.4 us
    pallas_call x1, Pallas kernels: 20.6 us -> 19.7 us  [body(): pl.pallas_call(functools.partial(kernel, n, z, width * z), out_shape=(plt...]
where the time goes in v3:
time: 21.2 us; the launch traced here: 21.1 us
  Pallas kernels  20.4 us (96%)
  between operations  0.64 us (3%)
    pallas_call x1, Pallas kernels, body(): pl.pallas_call(functools.partial(kernel, n, z, width * z), out_shape=(plt...  19.7 us
    pallas_call x1, Pallas kernels, body(): pl.pallas_call(settle, out_shape=tuple((jax.ShapeDtypeStruct(r.shape, r.d...  0.74 us

profile of v3, /device:TPU:0, one launch (start us, length us, event | category | flops | bytes accessed | tf_op | source)
XLA Modules:
  0.0 21.1 jit_solution(10806290996199611937)
XLA Ops:
  0.6 19.7 %shard_map.112 = (f32[8,8192]{1,0:T(8,128)S(1)}, f32[64,128]{1,0:T(8,128)S(1)}, f32[1,8]{1,0:T(1,128)S(1)}) custom-call(s32[1,128]{1,0:T(1,128)} %bitcast.9, s32[1,128]{1,0:T(1,128)} %bitcast.10, s32[1,128]{1,0:T(1,128)} %bitcast.11, bf16[64,128]{1,0:T(8,128)(2,1)} %bitcast.8, bf16[128,128]{1,0:T(8,128)(2,1)} %patch_hbm.1, f32[64,128]{1,0:T(8,128)} %bitcast.7, ...), custom_call_target="tpu_custom_call" | custom-call | tf_op jit(solution)/shard_map/pallas_call | solution.py:340
  20.3 0.7 %shard_map.113 = (f32[8,8192]{1,0:T(8,128)}, f32[64,128]{1,0:T(8,128)}, f32[1,8]{1,0:T(1,128)}) custom-call(f32[8,8192]{1,0:T(8,128)S(1)} %get-tuple-element.9.hess_in, f32[64,128]{1,0:T(8,128)S(1)} %get-tuple-element.10.diag_in, f32[1,8]{1,0:T(1,128)S(1)} %get-tuple-element.11.quad_in), custom_call_target="tpu_custom_call" | custom-call | tf_op jit(solution)/shard_map/pallas_call | solution.py:383

commit v4 on v3

--- a/solution.py
+++ b/solution.py
@@ -11,7 +11,7 @@
 BF16 = jnp.bfloat16
 NT = (((1,), (1,)), ((), ()))
 PARTS = 4
-CHUNKS = ((0, 1), (1, 2), (2, 4))
+ORDER = (0, 1, 3, 5, 2, 4, 6, 7)
 
 
 def kernel(
@@ -19,10 +19,10 @@
     owner_hbm, slot_hbm, count_hbm, obs_hbm, patch_hbm, sigma_hbm, probes_hbm, coef_hbm, op_hbm,
     hess_ref, diag_ref, quad_ref,
     index_ref, obs_ref, patch_ref, sigma_ref, probes_ref,
-    op_ref, ext_ref, ask_out, ask_in, row_out, row_in, value_ref, spread_ref, field_ref, sens_ref, hold_ref,
+    op_ref, ext_ref, ask_out, ask_in, row_out, row_in, keep_ref, value_ref, spread_ref, field_ref, sens_ref, hold_ref,
     diag_in, quad_in,
     load_sem, ask_send, ask_recv, row_send, row_recv, diag_send, diag_recv, quad_send, quad_recv,
-    answer,
+    answer, relay,
 ):
     width, nodes = probes_ref.shape
     blocks, vol = coef_hbm.shape
@@ -44,7 +44,7 @@
             bit *= 2
 
     def code(i):
-        return (0, 1, 2, 4, 3, 5, 6, 7)[i] if n == 8 else i
+        return ORDER[i] if n == len(ORDER) else i
 
     def flip(i):
         out = me
@@ -54,7 +54,10 @@
                     out = out + sign
         else:
             for b, sign in enumerate(signs):
-                out = out + sign * lax.rem(lax.div(i, jnp.int32(1 << b)), 2)
+                bits = lax.rem(lax.div(i, jnp.int32(1 << b)), 2)
+                if n == len(ORDER):
+                    bits = sum(jnp.where(i == k, code(k) >> b & 1, 0) for k in range(n))
+                out = out + sign * bits
         return out
 
     def peer_to(i):
@@ -88,7 +91,15 @@
 
     for i, src in enumerate((owner_hbm, slot_hbm)):
         pltpu.make_async_copy(src, index_ref.at[i], load_sem.at[0]).start()
-    each(1, n, greet)
+    far = n - 2 if n == len(ORDER) else n
+    upper = lax.div(me, 4) if n == len(ORDER) else 1
+    each(1, far, lambda i: greet(n - i))
+    if far < n:
+
+        @pl.when(upper == 0)
+        def _():
+            each(far, n, lambda i: greet(n - i))
+
     tell(barrier, zme + 1, z)
 
     smalls = ((count_hbm, index_ref.at[2]), (obs_hbm, obs_ref), (patch_hbm, patch_ref), (sigma_hbm, sigma_ref), (probes_hbm, probes_ref))
@@ -107,8 +118,10 @@
     rank = jnp.sum(jnp.where(same, 1.0, 0.0), axis=0, keepdims=True)
     key = owner * depth + rank
     turn = lax.div(down, depth)
-    if n == 8:
-        turn = jnp.where(turn == 3, 4, jnp.where(turn == 4, 3, turn))
+    if n == len(ORDER):
+        slot = turn
+        for i in range(n):
+            turn = jnp.where(slot == i, code(i), turn)
     if paired:
         turn = jnp.bitwise_xor(turn, me)
     else:
@@ -119,7 +132,7 @@
     asked = jnp.where(across == down, jnp.broadcast_to(asked, square), 0.0).astype(jnp.int32)
     ask_out[...] = jnp.sum(asked.reshape(n, depth, blocks), axis=1, keepdims=True)
 
-    pl.semaphore_wait(barrier, (n - 1) + zme)
+    pl.semaphore_wait(barrier, (far - 1) + (n - far) * upper + zme)
 
     def ask(i, part):
         return pltpu.make_async_remote_copy(
@@ -162,8 +175,22 @@
         )
 
     step = n // PARTS
-    for part in reversed(range(PARTS)):
-        each(max(part * step, 1), (part + 1) * step, lambda i: ask(i, part).start())
+
+    def ask_far():
+        each(far, n, lambda i: ask(i, i // step).start())
+
+    each(1, far, lambda i: ask(i, i // step if isinstance(i, int) else lax.div(i, step)).start())
+    if far < n:
+
+        @pl.when(upper == 1)
+        def _():
+            ask_far()
+
+        @pl.when((upper == 0) & (lax.rem(me, 2) == 1))
+        def _():
+            for i in (2, 4):
+                pl.semaphore_signal(relay, inc=1, device_id={"surf": peer_to(i)}, device_id_type=pl.DeviceIdType.MESH)
+
     tell(answer, 0, zme)
 
     for load in loads[:2]:
@@ -178,6 +205,7 @@
     counts = jnp.sum(jnp.where(chosen, counts, 0.0), axis=1, keepdims=True)
     keep_lane = lax.rem(lax.broadcasted_iota(jnp.int32, (blocks, patch), 1), cols).astype(F32)
     keep = jnp.where(keep_lane < counts, 1.0, 0.0)
+    keep_ref[...] = keep
     twice = (
         lax.rem(lax.broadcasted_iota(jnp.int32, (cols, patch), 1), cols)
         == lax.broadcasted_iota(jnp.int32, (cols, patch), 0)
@@ -208,64 +236,94 @@
 
     load_coef.wait()
 
+    ways = (0, 1 + lax.rem(me, 2), 2 - lax.rem(me, 2), 3)
+    extent = step * depth
+
+    def arrived(ref, sem, part):
+        if isinstance(part, int):
+            if (part + 1) * step > max(part * step, 1):
+                settled(ref.at[max(part * step, 1):(part + 1) * step], sem.at[part])
+        else:
+            settled(ref.at[pl.ds(part * step, step)], sem.at[part])
+
+    def start_of(part):
+        return part * extent if isinstance(part, int) else pl.multiple_of(part * extent, extent)
+
     def serve(part):
-        lo, hi = part * step, (part + 1) * step
-        if hi > max(lo, 1):
-            settled(ask_in.at[max(lo, 1):hi], ask_recv.at[part])
-        rows_of = (hi - lo) * depth
-        shape = (rows_of, blocks)
-        wanted = jnp.sum(ask_in[lo:hi], axis=0)
-        if lo == 0:
+        arrived(ask_in, ask_recv, part)
+        shape = (extent, blocks)
+        wanted = jnp.sum(ask_in[pl.ds(part * step, step)], axis=0)
+        if isinstance(part, int) and part == 0:
             wanted = wanted + ask_out[0]
         here = lax.broadcasted_iota(jnp.int32, shape, 1)
-        diagonal = here == lax.broadcasted_iota(jnp.int32, shape, 0) + lo * depth
+        diagonal = here == lax.broadcasted_iota(jnp.int32, shape, 0) + part * extent
         wanted = jnp.sum(jnp.where(diagonal, jnp.broadcast_to(wanted, shape).astype(F32), 0.0), axis=1, keepdims=True)
         pick = jnp.where(jnp.broadcast_to(wanted, shape) == here.astype(F32), 1.0, 0.0).astype(BF16)
         rows = jnp.dot(pick, ext_ref[...], preferred_element_type=F32).astype(BF16)
-        row_out[lo:hi] = rows.reshape(hi - lo, depth, rows.shape[1])
-        if lo == 0:
+        row_out[pl.ds(part * step, step)] = rows.reshape(step, depth, rows.shape[1])
+        if isinstance(part, int) and part == 0:
             row_in[0] = row_out[0]
-        each(max(lo, 1), hi, lambda i: row(i, part).start())
+            each(1, step, lambda i: row(i, part).start())
+        elif isinstance(part, int):
+            each(part * step, (part + 1) * step, lambda i: row(i, part).start())
+        else:
+            each(0, step, lambda i: row(part * step + i, part).start())
 
     ask_in[0] = jnp.zeros(ask_in.shape[1:], jnp.int32)
-    for part in range(PARTS):
+    for part in ways:
         serve(part)
+        if far < n and isinstance(part, int) and part == 0:
+
+            @pl.when(upper == 0)
+            def _():
+                pl.semaphore_wait(relay, 1)
+                ask_far()
+
     load_op.wait()
 
-    for first, last in CHUNKS:
-        if last == PARTS:
-
-            @pl.when(zme < z - 1)
-            def _():
-                pl.semaphore_wait(answer, z - 1 - zme)
-
-        for part in range(first, last):
-            if (part + 1) * step > max(part * step, 1):
-                settled(row_in.at[max(part * step, 1):(part + 1) * step], row_recv.at[part])
-        rows_of = (last - first) * step * depth
-        span = slice(first * step * depth, last * step * depth)
-        got = row_in[first * step:last * step].reshape(rows_of, row_in.shape[2])
+    def column(part):
+        got = row_in[pl.ds(part * step, step)].reshape(extent, row_in.shape[2])
         coef = got[:, :vol]
         weight = got[:, vol:].astype(F32)
         lifted = jnp.concatenate(
-            [jnp.concatenate([field_ref[p, span, :]] * tiles, axis=1) * coef for p in range(width)], axis=0
-        )
+            [jnp.concatenate([field_ref[p, pl.ds(start_of(part), extent), :]] * tiles, axis=1) * coef for p in range(width)],
+            axis=0,
+        )
+        weight = jnp.concatenate([weight] * tiles, axis=1)
         state = jnp.dot(lifted, op_ref[...], preferred_element_type=F32)
-        weight = jnp.concatenate([weight] * tiles, axis=1)
         weighted = jnp.concatenate(
-            [(state[p * rows_of:(p + 1) * rows_of] * weight).astype(BF16) for p in range(width)], axis=0
+            [(state[p * extent:(p + 1) * extent] * weight).astype(BF16) for p in range(width)], axis=0
         )
         adjoint = lax.dot_general(weighted, op_ref[...], NT, preferred_element_type=F32)
-        coef = coef.astype(F32)
+        return adjoint
+
+    def fold(part, adjoint):
+        coef = row_in[pl.ds(part * step, step)].reshape(extent, row_in.shape[2])[:, :vol].astype(F32)
+        span = pl.ds(start_of(part), extent)
+        keep = keep_ref[span, :]
         for p in range(width):
-            at = slice(p * rows_of, (p + 1) * rows_of)
+            at = slice(p * extent, (p + 1) * extent)
             total = None
             for t in range(tiles):
                 cut = slice(t * patch, (t + 1) * patch)
                 term = adjoint[at, cut] * coef[:, cut]
                 total = term if total is None else total + term
-            total = (total + pltpu.roll(total, cols, 1)) * keep[span]
+            total = (total + pltpu.roll(total, cols, 1)) * keep
             sens_ref[span, p * patch:(p + 1) * patch] = total.astype(BF16)
+
+    before = None
+    for part in ways:
+        arrived(row_in, row_recv, part)
+        if isinstance(part, int) and part == PARTS - 1:
+
+            @pl.when(zme < z - 1)
+            def _():
+                pl.semaphore_wait(answer, z - 1 - zme)
+
+        if before is not None:
+            fold(*before)
+        before = part, column(part)
+    fold(*before)
 
     split = jnp.dot(scatter, sens_ref[...], preferred_element_type=F32)
     scaled = []
@@ -358,6 +416,7 @@
                 pltpu.VMEM((n, 1, blocks), jnp.int32),
                 pltpu.VMEM((n, depth, vol + patch), BF16),
                 pltpu.VMEM((n, depth, vol + patch), BF16),
+                pltpu.VMEM((blocks, patch), F32),
                 pltpu.VMEM((groups * width, patch), F32),
                 pltpu.VMEM((groups * width, patch), F32),
                 pltpu.VMEM((width, blocks, patch), BF16),
@@ -374,6 +433,7 @@
                 pltpu.SemaphoreType.DMA,
                 pltpu.SemaphoreType.DMA,
                 pltpu.SemaphoreType.DMA,
+                pltpu.SemaphoreType.REGULAR,
                 pltpu.SemaphoreType.REGULAR,
             ],
             compiler_params=pltpu.CompilerParams(

time: 21.2 us -> 19.9 us (0.939)
  Pallas kernels: 20.4 us -> 19.1 us
    pallas_call x1, Pallas kernels: 19.7 us -> 18.4 us  [body(): pl.pallas_call(functools.partial(kernel, n, z, width * z), out_shape=(plt...]
where the time goes in v4:
time: 19.9 us; the launch traced here: 19.7 us
  Pallas kernels  19.1 us (96%)
  between operations  0.64 us (3%)
    pallas_call x1, Pallas kernels, body(): pl.pallas_call(functools.partial(kernel, n, z, width * z), out_shape=(plt...  18.4 us
    pallas_call x1, Pallas kernels, body(): pl.pallas_call(settle, out_shape=tuple((jax.ShapeDtypeStruct(r.shape, r.d...  0.74 us

profile of v4, /device:TPU:0, one launch (start us, length us, event | category | flops | bytes accessed | tf_op | source)
XLA Modules:
  0.0 19.7 jit_solution(12028257689862125192)
XLA Ops:
  0.6 18.4 %shard_map.112 = (f32[8,8192]{1,0:T(8,128)S(1)}, f32[64,128]{1,0:T(8,128)S(1)}, f32[1,8]{1,0:T(1,128)S(1)}) custom-call(s32[1,128]{1,0:T(1,128)} %bitcast.9, s32[1,128]{1,0:T(1,128)} %bitcast.10, s32[1,128]{1,0:T(1,128)} %bitcast.11, bf16[64,128]{1,0:T(8,128)(2,1)} %bitcast.8, bf16[128,128]{1,0:T(8,128)(2,1)} %patch_hbm.1, f32[64,128]{1,0:T(8,128)} %bitcast.7, ...), custom_call_target="tpu_custom_call" | custom-call | tf_op jit(solution)/shard_map/pallas_call | solution.py:398
  19.0 0.7 %shard_map.113 = (f32[8,8192]{1,0:T(8,128)}, f32[64,128]{1,0:T(8,128)}, f32[1,8]{1,0:T(1,128)}) custom-call(f32[8,8192]{1,0:T(8,128)S(1)} %get-tuple-element.9.hess_in, f32[64,128]{1,0:T(8,128)S(1)} %get-tuple-element.10.diag_in, f32[1,8]{1,0:T(1,128)S(1)} %get-tuple-element.11.quad_in), custom_call_target="tpu_custom_call" | custom-call | tf_op jit(solution)/shard_map/pallas_call | solution.py:443

commit v5 on v4

--- a/solution.py
+++ b/solution.py
@@ -311,15 +311,13 @@
             total = (total + pltpu.roll(total, cols, 1)) * keep
             sens_ref[span, p * patch:(p + 1) * patch] = total.astype(BF16)
 
+    @pl.when(zme < z - 1)
+    def _():
+        pl.semaphore_wait(answer, z - 1 - zme)
+
     before = None
     for part in ways:
         arrived(row_in, row_recv, part)
-        if isinstance(part, int) and part == PARTS - 1:
-
-            @pl.when(zme < z - 1)
-            def _():
-                pl.semaphore_wait(answer, z - 1 - zme)
-
         if before is not None:
             fold(*before)
         before = part, column(part)

time: 19.9 us -> 19.9 us (level)
  no operation moved by 1% of the time
where the time goes in v5:
time: 19.9 us; the launch traced here: 19.7 us
  Pallas kernels  19.1 us (96%)
  between operations  0.64 us (3%)
    pallas_call x1, Pallas kernels, body(): pl.pallas_call(functools.partial(kernel, n, z, width * z), out_shape=(plt...  18.4 us
    pallas_call x1, Pallas kernels, body(): pl.pallas_call(settle, out_shape=tuple((jax.ShapeDtypeStruct(r.shape, r.d...  0.74 us

profile of v5, /device:TPU:0, one launch (start us, length us, event | category | flops | bytes accessed | tf_op | source)
XLA Modules:
  0.0 19.7 jit_solution(12086616792102883610)
XLA Ops:
  0.6 18.4 %shard_map.112 = (f32[8,8192]{1,0:T(8,128)S(1)}, f32[64,128]{1,0:T(8,128)S(1)}, f32[1,8]{1,0:T(1,128)S(1)}) custom-call(s32[1,128]{1,0:T(1,128)} %bitcast.9, s32[1,128]{1,0:T(1,128)} %bitcast.10, s32[1,128]{1,0:T(1,128)} %bitcast.11, bf16[64,128]{1,0:T(8,128)(2,1)} %bitcast.8, bf16[128,128]{1,0:T(8,128)(2,1)} %patch_hbm.1, f32[64,128]{1,0:T(8,128)} %bitcast.7, ...), custom_call_target="tpu_custom_call" | custom-call | tf_op jit(solution)/shard_map/pallas_call | solution.py:396
  19.0 0.7 %shard_map.113 = (f32[8,8192]{1,0:T(8,128)}, f32[64,128]{1,0:T(8,128)}, f32[1,8]{1,0:T(1,128)}) custom-call(f32[8,8192]{1,0:T(8,128)S(1)} %get-tuple-element.9.hess_in, f32[64,128]{1,0:T(8,128)S(1)} %get-tuple-element.10.diag_in, f32[1,8]{1,0:T(1,128)S(1)} %get-tuple-element.11.quad_in), custom_call_target="tpu_custom_call" | custom-call | tf_op jit(solution)/shard_map/pallas_call | solution.py:441
